TPU v7x, 32 devices: a whole 2x2x4 slice. The times are simulated.
32 devices in a mesh: blk: 8 (over z, x), rows: 4 (over y, core).
Axes of the slice: x: 2, y: 2, z: 4, core: 2. Of those that a mesh axis runs over, the one named last changes fastest.
Arguments:
- columns: float32 [512, 16384], P('blk', 'rows'), may hold values from -100 to 100
- plan: int32 [3, 16], replicated, may hold values from 0 to 15, as said below
Outputs:
- swept: float32 [512, 16384], P('blk', 'rows')
- off_ratio: float32 [3], replicated
Inputs may be any that keep to these rules, and one draw needn't show every extreme that they name: `plan`: row s is a permutation of the 16 positions (position k is slot k % 2 of blk index k // 2). In each row there are a slot t and a number m of 1 to 7 such that the block in slot t of every blk index i goes to slot t of blk index (i + m) modulo 16 / 2, and every other block stays where it is.
All inputs are finite; a program needn't handle non-finite values. Where the computation divides by a largest or mean magnitude, that divisor is 1e-20 or more.
Results may differ from a plain program's by a relative error of at most 0.00011.
Values sent between devices are 32-bit elements; how exact they have to be, the bound alone decides.
No kernel may reach another device: no remote copies, remote signals or barrier semaphores. Data moves between devices by JAX's collectives and lax.ppermute only.
A program may use at most 64 MiB of HBM per device.

v0:
```python
from functools import partial
import jax
import jax.numpy as jnp
from jax import lax
from jax.sharding import PartitionSpec as P

STEPS = 3
EIG_ITERS = 3
NS_ITERS = 8
PRECISE = lax.Precision.HIGHEST


def shifted(value, axis, steps):
    count = lax.axis_size(axis)
    pairs = [(source, (source + steps) % count) for source in range(count)]
    return lax.ppermute(value, axis, pairs)


def matmul(left, right):
    return jnp.matmul(left, right, precision=PRECISE, preferred_element_type=jnp.float32)


def orthonormal(matrix):
    lengths = jnp.sqrt(jnp.sum(matrix * matrix, axis=0, keepdims=True))
    normed = matrix / lengths
    inner = matmul(normed.T, normed)
    bound = jnp.max(jnp.sum(jnp.abs(inner), axis=1))
    normed = normed / jnp.sqrt(bound)
    for turn_index in range(NS_ITERS):
        normed = 1.5 * normed - 0.5 * matmul(normed, matmul(normed.T, normed))
    return normed


def pair_rotation(gram_sum):
    rotation = jnp.eye(gram_sum.shape[0], dtype=gram_sum.dtype)
    for turn_index in range(EIG_ITERS):
        rotation = orthonormal(matmul(gram_sum, rotation))
    return rotation


def move_by(values, distance):
    return shifted(values, "blk", distance)


def local(columns, plan):
    block_width = columns.shape[0] // 2
    cycle_size = lax.axis_size("blk")
    eye_mask = jnp.eye(2 * block_width, dtype=bool)
    current = columns
    off_list = []
    diag_list = []
    for step_index in range(STEPS):
        partial_gram = matmul(current, current.T)
        gram_sum = lax.psum(partial_gram, "rows")
        off_part = jnp.where(eye_mask, 0.0, gram_sum)
        diag_part = jnp.where(eye_mask, gram_sum, 0.0)
        off_local = jnp.sum(off_part * off_part)
        diag_local = jnp.sum(diag_part * diag_part)
        off_total, diag_total = lax.psum((off_local, diag_local), "blk")
        off_list.append(off_total)
        diag_list.append(diag_total)
        rotation = pair_rotation(gram_sum)
        rotated = matmul(rotation.T, current)
        first_dest = plan[step_index, 0]
        second_dest = plan[step_index, 1]
        partner_step = jnp.maximum(first_dest // 2, second_dest // 2)
        leaving_high = second_dest != 1
        moving = jnp.where(leaving_high, rotated[block_width:], rotated[:block_width])
        staying = jnp.where(leaving_high, rotated[:block_width], rotated[block_width:])
        branches = [partial(move_by, distance=distance) for distance in range(1, cycle_size)]
        moving = lax.switch(partner_step - 1, branches, moving)
        current = jnp.where(
            leaving_high,
            jnp.concatenate([staying, moving], axis=0),
            jnp.concatenate([moving, staying], axis=0),
        )
    off_sums = jnp.stack(off_list)
    diag_sums = jnp.stack(diag_list)
    return (current, jnp.sqrt(off_sums) / jnp.sqrt(diag_sums))


def solution(mesh):
    return jax.shard_map(
        local,
        mesh=mesh,
        in_specs=(P("blk", "rows"), P()),
        out_specs=(P("blk", "rows"), P()),
        check_vma=False,
    )
```

profile of v0, /device:TPU:0, one launch (start us, length us, event | category | flops | bytes accessed | tf_op | source)
XLA Modules:
  0.0 189.1 jit_solution(8808458993383925959)
XLA Ops:
  0.6 1.6 fusion.124
  19.2 1.0 fusion.125
  20.2 12.9 %psum.63 = f32[64,64]{1,0:T(8,128)S(1)} all-reduce(f32[64,64]{1,0:T(8,128)S(1)} %fusion.125), channel_id=1, replica_groups=mesh['blk'=8,'rows'=4] {'rows'}, use_global_device_ids=true, to_apply=%region_0.0 | all-reduce | flops 4096 | bytes 32768 | tf_op jit(solution)/shard_map/psum | solution.py:54
  33.1 0.7 multiply_reduce_fusion.2
  34.0 0.3 fusion.72
  34.3 0.6 reduce_max.81
  35.6 0.2 fusion.110
  39.1 0.3 fusion.73
  39.3 0.6 reduce_max.82
  40.7 0.2 fusion.111
  44.2 0.3 fusion.74
  44.4 0.6 reduce_max.83
  45.7 0.2 fusion.112
  49.1 1.0 fusion.147
  50.2 13.9 %conditional.3 = (f32[32,4096]{1,0:T(8,128)}) conditional(s32[]{:T(128)} %clamp.9, f32[32,4096]{1,0:T(8,128)S(1)} %get-tuple-element.64, f32[32,4096]{1,0:T(8,128)S(1)} %get-tuple-element.64, f32[32,4096]{1,0:T(8,128)S(1)} %get-tuple-element.64, f32[32,4096]{1,0:T(8,128)S(1)} %get-tuple-element.64, ...), branch_computations={%region_10.11_spmd, %region_11.12_spmd, %region_12.13_spmd, %regio... | conditional | bytes 2097200 | solution.py:71
  50.2 3.7 %collective-permute-start.5 = (f32[32,4096]{1,0:T(8,128)S(1)}, f32[32,4096]{1,0:T(8,128)}, u32[]{:S(2)}, u32[]{:S(2)}) collective-permute-start(f32[32,4096]{1,0:T(8,128)S(1)} %param.5), channel_id=1, source_target_pairs={{0,24},{4,28},{8,0},{12,4},{16,8},{20,12},{24,16},{28,20},{1,25},{... | collective-permute-start | bytes 1572872 | tf_op jit(solution)/shard_map/cond/branch_5_fun/ppermute | solution.py:16
  53.9 10.2 %collective-permute-done.5 = f32[32,4096]{1,0:T(8,128)} collective-permute-done((f32[32,4096]{1,0:T(8,128)S(1)}, f32[32,4096]{1,0:T(8,128)}, u32[]{:S(2)}, u32[]{:S(2)}) %collective-permute-start.5) | collective-permute-done | bytes 524320 | tf_op jit(solution)/shard_map/cond/branch_5_fun/ppermute | solution.py:16
  64.0 2.7 %fusion.84 = f32[64,64]{1,0:T(8,128)S(1)} fusion(f32[32,4096]{1,0:T(8,128)} %get-tuple-element.89, f32[32,4096]{1,0:T(8,128)S(1)} %get-tuple-element.63, pred[]{:T(512)S(6)} %ne.49), kind=kOutput, calls=%fused_computation.168 | convolution fusion | flops 202113024 | bytes 1064961 | tf_op jit(solution)/shard_map/dot_general | solution.py:20
  66.8 10.7 %psum.64 = f32[64,64]{1,0:T(8,128)S(1)} all-reduce(f32[64,64]{1,0:T(8,128)S(1)} %fusion.84), channel_id=1, replica_groups=mesh['blk'=8,'rows'=4] {'rows'}, use_global_device_ids=true, to_apply=%region_17.18 | all-reduce | flops 4096 | bytes 32768 | tf_op jit(solution)/shard_map/psum | solution.py:54
  77.5 0.7 multiply_reduce_fusion.1
  78.3 0.3 fusion.75
  78.6 0.6 reduce_max.84
  83.4 0.3 fusion.76
  83.7 0.6 reduce_max.85
  88.5 0.3 fusion.77
  88.8 0.6 reduce_max.86
  93.4 2.3 %fusion.83 = f32[64,4096]{1,0:T(8,128)S(1)} fusion(f32[64,64]{1,0:T(8,128)S(1)} %fusion.24, f32[32,4096]{1,0:T(8,128)} %get-tuple-element.89, f32[32,4096]{1,0:T(8,128)S(1)} %get-tuple-element.63, pred[]{:T(512)S(6)} %ne.49), kind=kOutput, calls=%fused_computation.167 | convolution fusion | flops 202113024 | bytes 2113537 | tf_op jit(solution)/shard_map/dot_general | solution.py:20
  95.8 27.1 %conditional.4 = (f32[32,4096]{1,0:T(8,128)}) conditional(s32[]{:T(128)} %clamp.10, f32[32,4096]{1,0:T(8,128)S(1)} %get-tuple-element.62, f32[32,4096]{1,0:T(8,128)S(1)} %get-tuple-element.62, f32[32,4096]{1,0:T(8,128)S(1)} %get-tuple-element.62, f32[32,4096]{1,0:T(8,128)S(1)} %get-tuple-element.62, ...), branch_computations={%region_27.28_spmd, %region_28.29_spmd, %region_29.30_spmd, %regio... | conditional | bytes 2097200 | solution.py:71
  95.8 1.5 collective-permute-start.9
  97.4 25.6 %collective-permute-done.9 = f32[32,4096]{1,0:T(8,128)} collective-permute-done((f32[32,4096]{1,0:T(8,128)S(1)}, f32[32,4096]{1,0:T(8,128)}, u32[]{:S(2)}, u32[]{:S(2)}) %collective-permute-start.9) | collective-permute-done | bytes 524320 | tf_op jit(solution)/shard_map/cond/branch_2_fun/ppermute | solution.py:16
  122.9 2.7 %fusion.82 = f32[64,64]{1,0:T(8,128)S(1)} fusion(f32[32,4096]{1,0:T(8,128)} %get-tuple-element.90, f32[32,4096]{1,0:T(8,128)S(1)} %get-tuple-element.61, pred[]{:T(512)S(6)} %ne.48), kind=kOutput, calls=%fused_computation.166 | convolution fusion | flops 202113024 | bytes 1064961 | tf_op jit(solution)/shard_map/dot_general | solution.py:20
  125.7 10.3 %psum.65 = f32[64,64]{1,0:T(8,128)S(1)} all-reduce(f32[64,64]{1,0:T(8,128)S(1)} %fusion.82), channel_id=1, replica_groups=mesh['blk'=8,'rows'=4] {'rows'}, use_global_device_ids=true, to_apply=%region_34.35 | all-reduce | flops 4096 | bytes 32768 | tf_op jit(solution)/shard_map/psum | solution.py:54
  135.9 0.6 multiply_reduce_fusion
  136.6 18.0 %all-reduce = (f32[1]{0:T(128)}, f32[1]{0:T(128)}, f32[1]{0:T(128)}, f32[1]{0:T(128)}, f32[1]{0:T(128)}, /*index=5*/f32[1]{0:T(128)}) all-reduce(f32[1]{0:T(128)} %bitcast.8, f32[1]{0:T(128)} %bitcast.7, f32[1]{0:T(128)} %bitcast.6, f32[1]{0:T(128)} %bitcast.11, f32[1]{0:T(128)} %bitcast.10, ...), channel_id=1, replica_groups=mesh['blk'=8,'rows'=4] {'blk'}, use_global_device_ids=true, to_apply=%region_56.57 | all-reduce | flops 6 | bytes 48 | tf_op jit(solution)/shard_map/psum | solution.py:59
  154.6 4.3 %fusion.119 = f32[3]{0:T(128)} fusion(f32[1]{0:T(128)} %get-tuple-element.53, f32[1]{0:T(128)} %get-tuple-element.54, f32[1]{0:T(128)} %get-tuple-element.55, f32[1]{0:T(128)} %get-tuple-element.56, f32[1]{0:T(128)} %get-tuple-element.57, f32[1]{0:T(128)} %get-tuple-element.58), kind=kLoop, calls=%fused_computation.235 | loop fusion | flops 15 | bytes 36 | tf_op jit(solution)/shard_map/div | solution.py:79
  159.1 0.3 fusion.78
  159.4 0.6 reduce_max.87
  160.7 0.2 fusion.116
  164.2 0.3 fusion.79
  164.5 0.6 reduce_max.88
  165.8 0.2 fusion.117
  169.3 0.3 fusion.80
  169.6 0.6 reduce_max.89
  174.2 2.3 %fusion.81 = f32[64,4096]{1,0:T(8,128)S(1)} fusion(f32[64,64]{1,0:T(8,128)S(1)} %fusion, f32[32,4096]{1,0:T(8,128)} %get-tuple-element.90, f32[32,4096]{1,0:T(8,128)S(1)} %get-tuple-element.61, pred[]{:T(512)S(6)} %ne.48), kind=kOutput, calls=%fused_computation.165 | convolution fusion | flops 202113024 | bytes 2113537 | tf_op jit(solution)/shard_map/dot_general | solution.py:20
  176.6 10.3 %conditional.5 = (f32[32,4096]{1,0:T(8,128)}) conditional(s32[]{:T(128)} %clamp.11, f32[32,4096]{1,0:T(8,128)S(1)} %get-tuple-element.60, f32[32,4096]{1,0:T(8,128)S(1)} %get-tuple-element.60, f32[32,4096]{1,0:T(8,128)S(1)} %get-tuple-element.60, f32[32,4096]{1,0:T(8,128)S(1)} %get-tuple-element.60, ...), branch_computations={%region_44.45_spmd, %region_45.46_spmd, %region_46.47_spmd, %regio... | conditional | bytes 2097200 | solution.py:71
  176.6 2.1 %collective-permute-start.20 = (f32[32,4096]{1,0:T(8,128)S(1)}, f32[32,4096]{1,0:T(8,128)}, u32[]{:S(2)}, u32[]{:S(2)}) collective-permute-start(f32[32,4096]{1,0:T(8,128)S(1)} %param.20), channel_id=1, source_target_pairs={{0,28},{4,0},{8,4},{12,8},{16,12},{20,16},{24,20},{28,24},{1,29},{... | collective-permute-start | bytes 1572872 | tf_op jit(solution)/shard_map/cond/branch_6_fun/ppermute | solution.py:16
  178.7 8.2 %collective-permute-done.20 = f32[32,4096]{1,0:T(8,128)} collective-permute-done((f32[32,4096]{1,0:T(8,128)S(1)}, f32[32,4096]{1,0:T(8,128)}, u32[]{:S(2)}, u32[]{:S(2)}) %collective-permute-start.20) | collective-permute-done | bytes 524320 | tf_op jit(solution)/shard_map/cond/branch_6_fun/ppermute | solution.py:16
  186.8 2.3 %maximum_select_fusion.2 = f32[64,4096]{1,0:T(8,128)} fusion(f32[32,4096]{1,0:T(8,128)} %get-tuple-element.91, f32[32,4096]{1,0:T(8,128)S(1)} %get-tuple-element.59, pred[]{:T(512)S(6)} %ne.47), kind=kLoop, calls=%fused_computation.164 | loop fusion | flops 786432 | bytes 2097153 | tf_op jit(solution)/shard_map/jit(_where)/select_n | solution.py:72
  (171 shorter events, 29.4 us)
Async XLA Ops:
  0.6 18.6 %copy-start = (f32[64,4096]{1,0:T(8,128)S(1)}, f32[64,4096]{1,0:T(8,128)}, u32[]{:S(2)}) copy-start(f32[64,4096]{1,0:T(8,128)} %param.23) | copy-start | bytes 3145732
  50.2 13.8 %collective-permute-start.5 = (f32[32,4096]{1,0:T(8,128)S(1)}, f32[32,4096]{1,0:T(8,128)}, u32[]{:S(2)}, u32[]{:S(2)}) collective-permute-start(f32[32,4096]{1,0:T(8,128)S(1)} %param.5), channel_id=1, source_target_pairs={{0,24},{4,28},{8,0},{12,4},{16,8},{20,12},{24,16},{28,20},{1,25},{... | collective-permute-start | bytes 1572872 | tf_op jit(solution)/shard_map/cond/branch_5_fun/ppermute | solution.py:16
  95.8 27.1 %collective-permute-start.9 = (f32[32,4096]{1,0:T(8,128)S(1)}, f32[32,4096]{1,0:T(8,128)}, u32[]{:S(2)}, u32[]{:S(2)}) collective-permute-start(f32[32,4096]{1,0:T(8,128)S(1)} %param.9), channel_id=1, source_target_pairs={{0,12},{4,16},{8,20},{12,24},{16,28},{20,0},{24,4},{28,8},{1,13},{... | collective-permute-start | bytes 1572872 | tf_op jit(solution)/shard_map/cond/branch_2_fun/ppermute | solution.py:16
  176.6 10.2 %collective-permute-start.20 = (f32[32,4096]{1,0:T(8,128)S(1)}, f32[32,4096]{1,0:T(8,128)}, u32[]{:S(2)}, u32[]{:S(2)}) collective-permute-start(f32[32,4096]{1,0:T(8,128)S(1)} %param.20), channel_id=1, source_target_pairs={{0,28},{4,0},{8,4},{12,8},{16,12},{20,16},{24,20},{28,24},{1,29},{... | collective-permute-start | bytes 1572872 | tf_op jit(solution)/shard_map/cond/branch_6_fun/ppermute | solution.py:16
where the time goes:
time: 190 us; the launch traced here: 189 us
  blocking collectives  51.9 us (27%)
  matrix products  44.7 us (24%)
  waiting for transfers between devices  43.9 us (23%)
  between operations  25.2 us (13%)
  other arithmetic  14.3 us (8%)
  starting transfers between devices  7.26 us (4%)
    dot_general x168, matrix products, matmul(): jnp.matmul(left, right, precision=PRECISE, preferred_element_type=jnp.flo...  44.7 us
    ppermute x3, waiting for transfers between devices, shifted(): return lax.ppermute(value, axis, pairs)  43.9 us
    psum x3, blocking collectives, local(): gram_sum = lax.psum(partial_gram, 'rows')  33.9 us
    psum x1, blocking collectives, local(): off_total, diag_total = lax.psum((off_local, diag_local), 'blk')  18 us
    ppermute x3, starting transfers between devices, shifted(): return lax.ppermute(value, axis, pairs)  7.26 us
    reduce_max x9, other arithmetic, orthonormal(): bound = jnp.max(jnp.sum(jnp.abs(inner), axis=1))  5.47 us
    div x1, other arithmetic, local(): return (current, jnp.sqrt(off_sums) / jnp.sqrt(diag_sums))  4.33 us
  transfers between devices with their start and end apart: 3, of which 3 were waited for; matrix products, arithmetic and copies ran while one was open for 0% of the time, Pallas kernels for 0%

commit v1 on v0

--- a/solution.py
+++ b/solution.py
@@ -51,7 +51,7 @@
     diag_list = []
     for step_index in range(STEPS):
         partial_gram = matmul(current, current.T)
-        gram_sum = lax.psum(partial_gram, "rows")
+        gram_sum = jnp.sum(lax.all_gather(partial_gram, "rows"), axis=0)
         off_part = jnp.where(eye_mask, 0.0, gram_sum)
         diag_part = jnp.where(eye_mask, gram_sum, 0.0)
         off_local = jnp.sum(off_part * off_part)

time: 190 us -> 176 us (0.926)
  blocking collectives: 51.9 us -> 35.6 us
  waiting for transfers between devices: 43.9 us -> 46.3 us
    psum x3 -> x0, blocking collectives: 33.9 us -> none  [local(): gram_sum = lax.psum(partial_gram, 'rows')]
    all_gather x0 -> x3, blocking collectives: none -> 17.6 us  [local(): gram_sum = jnp.sum(lax.all_gather(partial_gram, 'rows'), axis=0)]
    ppermute x3, waiting for transfers between devices: 43.9 us -> 46.3 us  [shifted(): return lax.ppermute(value, axis, pairs)]
where the time goes in v1:
time: 176 us; the launch traced here: 175 us
  waiting for transfers between devices  46.3 us (26%)
  matrix products  44.7 us (25%)
  blocking collectives  35.6 us (20%)
  between operations  25.2 us (14%)
  other arithmetic  14.4 us (8%)
  starting transfers between devices  7.61 us (4%)
    ppermute x3, waiting for transfers between devices, shifted(): return lax.ppermute(value, axis, pairs)  46.3 us
    dot_general x168, matrix products, matmul(): jnp.matmul(left, right, precision=PRECISE, preferred_element_type=jnp.flo...  44.7 us
    psum x1, blocking collectives, local(): off_total, diag_total = lax.psum((off_local, diag_local), 'blk')  18 us
    all_gather x3, blocking collectives, local(): gram_sum = jnp.sum(lax.all_gather(partial_gram, 'rows'), axis=0)  17.6 us
    ppermute x3, starting transfers between devices, shifted(): return lax.ppermute(value, axis, pairs)  7.61 us
    reduce_max x9, other arithmetic, orthonormal(): bound = jnp.max(jnp.sum(jnp.abs(inner), axis=1))  5.47 us
    div x1, other arithmetic, local(): return (current, jnp.sqrt(off_sums) / jnp.sqrt(diag_sums))  4.33 us
  transfers between devices with their start and end apart: 3, of which 3 were waited for; matrix products, arithmetic and copies ran while one was open for 0% of the time, Pallas kernels for 0%

profile of v1, /device:TPU:0, one launch (start us, length us, event | category | flops | bytes accessed | tf_op | source)
XLA Modules:
  0.0 175.5 jit_solution(11053742610367515310)
XLA Ops:
  0.6 1.6 fusion.124
  19.2 1.0 fusion.125
  20.2 6.5 %all-gather = f32[256,64]{1,0:T(8,128)S(1)} all-gather(f32[64,64]{1,0:T(8,128)S(1)} %fusion.125), channel_id=2, replica_groups=mesh['blk'=8,'rows'=4] {'rows'}, dimensions={0}, use_global_device_ids=true | all-gather | bytes 81920 | tf_op jit(solution)/shard_map/all_gather | solution.py:54
  26.7 0.7 multiply_reduce_fusion.2
  27.6 0.3 fusion.72
  27.9 0.6 reduce_max.81
  29.2 0.2 fusion.110
  32.7 0.3 fusion.73
  33.0 0.6 reduce_max.82
  37.8 0.3 fusion.74
  38.1 0.6 reduce_max.83
  39.4 0.2 fusion.112
  42.7 1.0 fusion.147
  43.8 15.7 %conditional.3 = (f32[32,4096]{1,0:T(8,128)}) conditional(s32[]{:T(128)} %clamp.9, f32[32,4096]{1,0:T(8,128)S(1)} %get-tuple-element.64, f32[32,4096]{1,0:T(8,128)S(1)} %get-tuple-element.64, f32[32,4096]{1,0:T(8,128)S(1)} %get-tuple-element.64, f32[32,4096]{1,0:T(8,128)S(1)} %get-tuple-element.64, ...), branch_computations={%region_10.11_spmd, %region_11.12_spmd, %region_12.13_spmd, %regio... | conditional | bytes 2097200 | solution.py:71
  43.8 4.0 %collective-permute-start.5 = (f32[32,4096]{1,0:T(8,128)S(1)}, f32[32,4096]{1,0:T(8,128)}, u32[]{:S(2)}, u32[]{:S(2)}) collective-permute-start(f32[32,4096]{1,0:T(8,128)S(1)} %param.5), channel_id=1, source_target_pairs={{0,24},{4,28},{8,0},{12,4},{16,8},{20,12},{24,16},{28,20},{1,25},{... | collective-permute-start | bytes 1572872 | tf_op jit(solution)/shard_map/cond/branch_5_fun/ppermute | solution.py:16
  47.8 11.7 %collective-permute-done.5 = f32[32,4096]{1,0:T(8,128)} collective-permute-done((f32[32,4096]{1,0:T(8,128)S(1)}, f32[32,4096]{1,0:T(8,128)}, u32[]{:S(2)}, u32[]{:S(2)}) %collective-permute-start.5) | collective-permute-done | bytes 524320 | tf_op jit(solution)/shard_map/cond/branch_5_fun/ppermute | solution.py:16
  59.5 2.7 %fusion.84 = f32[64,64]{1,0:T(8,128)S(1)} fusion(f32[32,4096]{1,0:T(8,128)} %get-tuple-element.89, f32[32,4096]{1,0:T(8,128)S(1)} %get-tuple-element.63, pred[]{:T(512)S(6)} %ne.49), kind=kOutput, calls=%fused_computation.168 | convolution fusion | flops 202113024 | bytes 1064961 | tf_op jit(solution)/shard_map/dot_general | solution.py:20
  62.3 5.6 %all-gather.1 = f32[256,64]{1,0:T(8,128)S(1)} all-gather(f32[64,64]{1,0:T(8,128)S(1)} %fusion.84), channel_id=3, replica_groups=mesh['blk'=8,'rows'=4] {'rows'}, dimensions={0}, use_global_device_ids=true | all-gather | bytes 81920 | tf_op jit(solution)/shard_map/all_gather | solution.py:54
  67.9 0.7 multiply_reduce_fusion.1
  68.7 0.3 fusion.75
  69.0 0.6 reduce_max.84
  73.8 0.3 fusion.76
  74.1 0.6 reduce_max.85
  75.4 0.2 fusion.114
  78.9 0.3 fusion.77
  79.2 0.6 reduce_max.86
  83.8 2.3 %fusion.83 = f32[64,4096]{1,0:T(8,128)S(1)} fusion(f32[64,64]{1,0:T(8,128)S(1)} %fusion.24, f32[32,4096]{1,0:T(8,128)} %get-tuple-element.89, f32[32,4096]{1,0:T(8,128)S(1)} %get-tuple-element.63, pred[]{:T(512)S(6)} %ne.49), kind=kOutput, calls=%fused_computation.167 | convolution fusion | flops 202113024 | bytes 2113537 | tf_op jit(solution)/shard_map/dot_general | solution.py:20
  86.2 27.4 %conditional.4 = (f32[32,4096]{1,0:T(8,128)}) conditional(s32[]{:T(128)} %clamp.10, f32[32,4096]{1,0:T(8,128)S(1)} %get-tuple-element.62, f32[32,4096]{1,0:T(8,128)S(1)} %get-tuple-element.62, f32[32,4096]{1,0:T(8,128)S(1)} %get-tuple-element.62, f32[32,4096]{1,0:T(8,128)S(1)} %get-tuple-element.62, ...), branch_computations={%region_27.28_spmd, %region_28.29_spmd, %region_29.30_spmd, %regio... | conditional | bytes 2097200 | solution.py:71
  86.2 1.5 collective-permute-start.9
  87.8 25.8 %collective-permute-done.9 = f32[32,4096]{1,0:T(8,128)} collective-permute-done((f32[32,4096]{1,0:T(8,128)S(1)}, f32[32,4096]{1,0:T(8,128)}, u32[]{:S(2)}, u32[]{:S(2)}) %collective-permute-start.9) | collective-permute-done | bytes 524320 | tf_op jit(solution)/shard_map/cond/branch_2_fun/ppermute | solution.py:16
  113.6 2.7 %fusion.82 = f32[64,64]{1,0:T(8,128)S(1)} fusion(f32[32,4096]{1,0:T(8,128)} %get-tuple-element.90, f32[32,4096]{1,0:T(8,128)S(1)} %get-tuple-element.61, pred[]{:T(512)S(6)} %ne.48), kind=kOutput, calls=%fused_computation.166 | convolution fusion | flops 202113024 | bytes 1064961 | tf_op jit(solution)/shard_map/dot_general | solution.py:20
  116.3 5.4 %all-gather.2 = f32[256,64]{1,0:T(8,128)S(1)} all-gather(f32[64,64]{1,0:T(8,128)S(1)} %fusion.82), channel_id=4, replica_groups=mesh['blk'=8,'rows'=4] {'rows'}, dimensions={0}, use_global_device_ids=true | all-gather | bytes 81920 | tf_op jit(solution)/shard_map/all_gather | solution.py:54
  121.7 0.6 multiply_reduce_fusion
  122.3 18.0 %all-reduce = (f32[1]{0:T(128)}, f32[1]{0:T(128)}, f32[1]{0:T(128)}, f32[1]{0:T(128)}, f32[1]{0:T(128)}, /*index=5*/f32[1]{0:T(128)}) all-reduce(f32[1]{0:T(128)} %bitcast.11, f32[1]{0:T(128)} %bitcast.10, f32[1]{0:T(128)} %bitcast.9, f32[1]{0:T(128)} %bitcast.14, f32[1]{0:T(128)} %bitcast.13, ...), channel_id=1, replica_groups=mesh['blk'=8,'rows'=4] {'blk'}, use_global_device_ids=true, to_apply=%region_56.57 | all-reduce | flops 6 | bytes 48 | tf_op jit(solution)/shard_map/psum | solution.py:59
  140.4 4.3 %fusion.119 = f32[3]{0:T(128)} fusion(f32[1]{0:T(128)} %get-tuple-element.53, f32[1]{0:T(128)} %get-tuple-element.54, f32[1]{0:T(128)} %get-tuple-element.55, f32[1]{0:T(128)} %get-tuple-element.56, f32[1]{0:T(128)} %get-tuple-element.57, f32[1]{0:T(128)} %get-tuple-element.58), kind=kLoop, calls=%fused_computation.235 | loop fusion | flops 15 | bytes 36 | tf_op jit(solution)/shard_map/div | solution.py:79
  144.9 0.3 fusion.78
  145.2 0.6 reduce_max.87
  146.5 0.2 fusion.116
  150.0 0.3 fusion.79
  150.3 0.6 reduce_max.88
  155.1 0.3 fusion.80
  155.3 0.6 reduce_max.89
  156.7 0.2 fusion.118
  160.0 2.3 %fusion.81 = f32[64,4096]{1,0:T(8,128)S(1)} fusion(f32[64,64]{1,0:T(8,128)S(1)} %fusion, f32[32,4096]{1,0:T(8,128)} %get-tuple-element.90, f32[32,4096]{1,0:T(8,128)S(1)} %get-tuple-element.61, pred[]{:T(512)S(6)} %ne.48), kind=kOutput, calls=%fused_computation.165 | convolution fusion | flops 202113024 | bytes 2113537 | tf_op jit(solution)/shard_map/dot_general | solution.py:20
  162.3 10.9 %conditional.5 = (f32[32,4096]{1,0:T(8,128)}) conditional(s32[]{:T(128)} %clamp.11, f32[32,4096]{1,0:T(8,128)S(1)} %get-tuple-element.60, f32[32,4096]{1,0:T(8,128)S(1)} %get-tuple-element.60, f32[32,4096]{1,0:T(8,128)S(1)} %get-tuple-element.60, f32[32,4096]{1,0:T(8,128)S(1)} %get-tuple-element.60, ...), branch_computations={%region_44.45_spmd, %region_45.46_spmd, %region_46.47_spmd, %regio... | conditional | bytes 2097200 | solution.py:71
  162.4 2.1 %collective-permute-start.20 = (f32[32,4096]{1,0:T(8,128)S(1)}, f32[32,4096]{1,0:T(8,128)}, u32[]{:S(2)}, u32[]{:S(2)}) collective-permute-start(f32[32,4096]{1,0:T(8,128)S(1)} %param.20), channel_id=1, source_target_pairs={{0,28},{4,0},{8,4},{12,8},{16,12},{20,16},{24,20},{28,24},{1,29},{... | collective-permute-start | bytes 1572872 | tf_op jit(solution)/shard_map/cond/branch_6_fun/ppermute | solution.py:16
  164.4 8.8 %collective-permute-done.20 = f32[32,4096]{1,0:T(8,128)} collective-permute-done((f32[32,4096]{1,0:T(8,128)S(1)}, f32[32,4096]{1,0:T(8,128)}, u32[]{:S(2)}, u32[]{:S(2)}) %collective-permute-start.20) | collective-permute-done | bytes 524320 | tf_op jit(solution)/shard_map/cond/branch_6_fun/ppermute | solution.py:16
  173.2 2.3 %maximum_select_fusion.2 = f32[64,4096]{1,0:T(8,128)} fusion(f32[32,4096]{1,0:T(8,128)} %get-tuple-element.91, f32[32,4096]{1,0:T(8,128)S(1)} %get-tuple-element.59, pred[]{:T(512)S(6)} %ne.47), kind=kLoop, calls=%fused_computation.164 | loop fusion | flops 786432 | bytes 2097153 | tf_op jit(solution)/shard_map/jit(_where)/select_n | solution.py:72
  (174 shorter events, 29.5 us)
Async XLA Ops:
  0.6 18.6 %copy-start = (f32[64,4096]{1,0:T(8,128)S(1)}, f32[64,4096]{1,0:T(8,128)}, u32[]{:S(2)}) copy-start(f32[64,4096]{1,0:T(8,128)} %param.23) | copy-start | bytes 3145732
  43.8 15.7 %collective-permute-start.5 = (f32[32,4096]{1,0:T(8,128)S(1)}, f32[32,4096]{1,0:T(8,128)}, u32[]{:S(2)}, u32[]{:S(2)}) collective-permute-start(f32[32,4096]{1,0:T(8,128)S(1)} %param.5), channel_id=1, source_target_pairs={{0,24},{4,28},{8,0},{12,4},{16,8},{20,12},{24,16},{28,20},{1,25},{... | collective-permute-start | bytes 1572872 | tf_op jit(solution)/shard_map/cond/branch_5_fun/ppermute | solution.py:16
  86.2 27.4 %collective-permute-start.9 = (f32[32,4096]{1,0:T(8,128)S(1)}, f32[32,4096]{1,0:T(8,128)}, u32[]{:S(2)}, u32[]{:S(2)}) collective-permute-start(f32[32,4096]{1,0:T(8,128)S(1)} %param.9), channel_id=1, source_target_pairs={{0,12},{4,16},{8,20},{12,24},{16,28},{20,0},{24,4},{28,8},{1,13},{... | collective-permute-start | bytes 1572872 | tf_op jit(solution)/shard_map/cond/branch_2_fun/ppermute | solution.py:16
  162.4 10.9 %collective-permute-start.20 = (f32[32,4096]{1,0:T(8,128)S(1)}, f32[32,4096]{1,0:T(8,128)}, u32[]{:S(2)}, u32[]{:S(2)}) collective-permute-start(f32[32,4096]{1,0:T(8,128)S(1)} %param.20), channel_id=1, source_target_pairs={{0,28},{4,0},{8,4},{12,8},{16,12},{20,16},{24,20},{28,24},{1,29},{... | collective-permute-start | bytes 1572872 | tf_op jit(solution)/shard_map/cond/branch_6_fun/ppermute | solution.py:16
